TPU v7x, 32 devices: a whole 2x2x4 slice. The times are simulated.
32 devices in a mesh: asset: 8 (over z, y), tm: 4 (over x, core).
Axes of the slice: x: 2, y: 2, z: 4, core: 2. Of those that a mesh axis runs over, the one named last changes fastest.
Arguments:
- values: float32 [4, 1024, 16384], P(None, 'tm', 'asset'), may hold values from -64 to 64
- listed_from: int32 [16384], P('asset'), may hold values from -1024 to 1023, as said below
- listed_until: int32 [16384], P('asset'), may hold values from -960 to 3070, as said below
Outputs:
- standardized: float32 [4, 1024, 16384], P(None, 'tm', 'asset')
Inputs may be any that keep to these rules, and one draw needn't show every extreme that they name: listed_until[a] - listed_from[a] is at least 64. listed_until[a] - listed_from[a] is at least 64.
All inputs are finite; a program needn't handle non-finite values.
Results may differ from a plain program's by a relative error of at most 0.00005.
Values sent between devices are 32-bit elements; how exact they have to be, the bound alone decides.
A program may use at most 128 MiB of HBM per device.

v0:
```python
import jax
import jax.numpy as jnp
from jax import lax
from jax.sharding import PartitionSpec as P

WINDOW = 64


def passed_along(block, axis, distance):
    devices = range(lax.axis_size(axis))
    route = [(i - distance, i) for i in devices if i - distance in devices]
    return lax.ppermute(block, axis, route)


def listing(stamps, listed_from, listed_until):
    opened = listed_from[None, :]
    closed = listed_until[None, :]
    weight = ((stamps >= opened) & (stamps < closed)).astype(jnp.float32)
    window_low = jnp.maximum(jnp.maximum(stamps - (WINDOW - 1), opened), 0)
    window_high = jnp.minimum(stamps, closed - 1)
    counted = jnp.maximum(window_high - window_low + 1, 1)
    return (weight, counted.astype(jnp.float32))


def window_sums(masked):
    field_count, row_count, asset_count = masked.shape
    blocks = row_count // WINDOW
    current = masked.reshape(field_count, blocks, WINDOW, asset_count)
    offset = jnp.arange(WINDOW, dtype=jnp.int32)
    lower_band = (offset[None, :] <= offset[:, None]).astype(jnp.float32)
    upper_band = (offset[None, :] > offset[:, None]).astype(jnp.float32)
    highest = lax.Precision.HIGHEST
    within = jnp.einsum("ij,fbja->fbia", lower_band, current, precision=highest)
    tail_rows = passed_along(masked[:, row_count - WINDOW :], "tm", 1)
    carried = jnp.einsum("ij,fja->fia", upper_band, tail_rows, precision=highest)
    earlier = jnp.einsum("ij,fbja->fbia", upper_band, current[:, : blocks - 1], precision=highest)
    spread_in = jnp.concatenate([carried[:, None], earlier], axis=1)
    return (within + spread_in).reshape(field_count, row_count, asset_count)


def standardize(field_values, weight, count_part, count_total):
    local_sum = jnp.sum(field_values * weight[None], axis=2)
    local_sq = jnp.sum(weight[None] * field_values * field_values, axis=2)
    if count_total is None:
        count_total, totals, squares = lax.psum((count_part, local_sum, local_sq), "asset")
    else:
        totals, squares = lax.psum((local_sum, local_sq), "asset")
    count_floor = jnp.maximum(count_total, 1.0)[None, :]
    center = totals / count_floor
    spread = jnp.maximum(squares / count_floor - center * center, 0.0)
    deviate = (field_values - center[:, :, None]) * weight[None]
    return (deviate / jnp.sqrt(spread + 0.1)[:, :, None], count_total)


def per_device(values, listed_from, listed_until):
    field_count, row_count, asset_count = values.shape
    stamps = lax.axis_index("tm") * row_count + lax.broadcasted_iota(
        jnp.int32, (row_count, asset_count), 0
    )
    weight, counted = listing(stamps, listed_from, listed_until)
    masked = values * weight[None]
    rolling = window_sums(masked) / counted[None]
    count_part = jnp.sum(weight, axis=1)
    scored, count_total = standardize(rolling, weight, count_part, None)
    clipped = jnp.clip(scored, -3.0, 3.0)
    result_field, unused = standardize(clipped, weight, None, count_total)
    return result_field


def solution(mesh):
    in_specs = (P(None, "tm", "asset"), P("asset"), P("asset"))
    out_specs = P(None, "tm", "asset")
    return jax.shard_map(
        per_device, mesh=mesh, in_specs=in_specs, out_specs=out_specs, check_vma=False
    )
```

profile of v0, /device:TPU:6, one launch (start us, length us, event | category | flops | bytes accessed | tf_op | source)
XLA Modules:
  0.0 103.5 jit_solution(14459305484572161796)
XLA Ops:
  0.0 1.1 %and_convert_fusion.1 = f32[256,2048]{1,0:T(8,128)S(1)} fusion(s32[2048]{0:T(1024)} %param.5, s32[2048]{0:T(1024)} %param.4, s32[256]{0:T(256)S(1)} %iota_add_fusion), kind=kLoop, calls=%fused_computation.23 | loop fusion | flops 2097152 | bytes 2114560 | tf_op jit(solution)/shard_map/convert_element_type | solution.py:18
  1.1 0.0 copy-start.3
  1.1 0.0 copy-start.2
  1.1 5.4 %broadcast_multiply_fusion = f32[4,256,2048]{2,1,0:T(8,128)S(1)} fusion(f32[4,256,2048]{2,1,0:T(8,128)} %param.3, f32[256,2048]{1,0:T(8,128)S(1)} %and_convert_fusion.1), kind=kLoop, calls=%fused_computation.17 | loop fusion | flops 2097152 | bytes 18874368 | tf_op jit(solution)/shard_map/mul | solution.py:61
  6.6 0.2 slice.8
  6.8 1.9 %collective-permute-start = (f32[4,64,2048]{2,1,0:T(8,128)S(1)}, f32[4,64,2048]{2,1,0:T(8,128)S(1)}, u32[]{:S(2)}, u32[]{:S(2)}) collective-permute-start(f32[4,64,2048]{2,1,0:T(8,128)S(1)} %slice.8), channel_id=1, source_target_pairs={{0,1},{1,2},{2,3},{4,5},{5,6},{6,7},{8,9},{9,10},{10,11},{12,13},{... | collective-permute-start | bytes 6291464 | tf_op jit(solution)/shard_map/ppermute | solution.py:12
  8.8 0.5 fusion.9
  9.3 0.4 and_convert_fusion
  9.6 2.2 %maximum_convert_fusion.1 = f32[256,2048]{1,0:T(8,128)} fusion(s32[256]{0:T(256)S(1)} %broadcast_add_fusion.2, s32[2048]{0:T(1024)S(1)} %broadcast_add_fusion, s32[2048]{0:T(1024)S(1)} %copy-done.2, s32[256]{0:T(256)S(1)} %iota_add_fusion), kind=kLoop, calls=%fused_computation.21 | loop fusion | flops 3670016 | bytes 2115584 | tf_op jit(solution)/shard_map/convert_element_type | solution.py:22
  11.9 0.8 maximum_convert_fusion
  12.7 6.3 %convolution_bitcast_fusion = f32[4,3,64,2048]{3,2,1,0:T(8,128)} fusion(f32[4,4,64,2048]{3,2,1,0:T(8,128)S(1)} %bitcast.43), kind=kOutput, calls=%fused_computation.18 | convolution fusion | flops 1207963648 | bytes 14680064 | tf_op jit(solution)/shard_map/ij,fbja->fbia/dot_general | solution.py:36
  19.0 15.1 %collective-permute-done = f32[4,64,2048]{2,1,0:T(8,128)S(1)} collective-permute-done((f32[4,64,2048]{2,1,0:T(8,128)S(1)}, f32[4,64,2048]{2,1,0:T(8,128)S(1)}, u32[]{:S(2)}, u32[]{:S(2)}) %collective-permute-start) | collective-permute-done | bytes 2097184 | tf_op jit(solution)/shard_map/ppermute | solution.py:12
  34.1 1.4 %convolution_bitcast_fusion.1 = f32[4,1,64,2048]{3,2,1,0:T(8,128)S(1)} fusion(f32[4,64,2048]{2,1,0:T(8,128)S(1)} %collective-permute-done), kind=kOutput, calls=%fused_computation.19 | convolution fusion | flops 402657280 | bytes 4194304 | tf_op jit(solution)/shard_map/ij,fja->fia/dot_general | solution.py:35
  35.5 12.8 %multiply_reduce_fusion.1 = (f32[4,4,64]{2,1,0:T(4,128)S(1)}, f32[4,4,64]{2,1,0:T(4,128)S(1)}, f32[4,4,64,2048]{3,2,1,0:T(8,128)}) fusion(f32[4,64,2048]{2,1,0:T(8,128)S(1)} %and_convert_fusion, f32[4,64,2048]{2,1,0:T(8,128)S(1)} %maximum_convert_fusion, f32[4,3,64,2048]{3,2,1,0:T(8,128)} %convolution_bitcast_fusion, ...), kind=kOutput, calls=%fused_computation.3 | convolution fusion | flops 1625294848 | bytes 29368320 | tf_op jit(solution)/shard_map/ij,fbja->fbia/dot_general | solution.py:33
  48.3 0.1 reduce_sum.54
  48.4 0.1 reduce_sum.57
  48.5 18.6 %all-reduce.1 = (f32[4,256]{1,0:T(4,128)S(1)}, f32[256]{0:T(256)S(1)}, f32[4,256]{1,0:T(4,128)S(1)}) all-reduce(f32[4,256]{1,0:T(4,128)S(1)} %reduce_sum.57, f32[256]{0:T(256)S(1)} %fusion.9, f32[4,256]{1,0:T(4,128)S(1)} %reduce_sum.54), channel_id=1, replica_groups=mesh['asset'=8,'tm'=4] {'asset'}, use_global_device_ids=true, to_apply=%region_5.0 | all-reduce | flops 2304 | bytes 18432 | tf_op jit(solution)/shard_map/psum | solution.py:45
  67.1 0.1 div.75
  67.2 0.1 sub.59
  67.3 6.6 %multiply_reduce_fusion = (f32[4,4,64]{2,1,0:T(4,128)S(1)}, f32[4,4,64]{2,1,0:T(4,128)S(1)}) fusion(f32[4,64,2048]{2,1,0:T(8,128)S(1)} %and_convert_fusion, f32[4,4,64]{2,1,0:T(4,128)S(1)} %div.75, f32[4,4,64]{2,1,0:T(4,128)S(1)} %sub.59, f32[4,4,64,2048]{3,2,1,0:T(8,128)} %get-tuple-element.18, f32[4,64,2048]{2,1,0:T(8,128)} %copy-done), kind=kLoop, calls=%fused_computation.1 | loop fusion | flops 18872320 | bytes 12599296 | tf_op jit(solution)/shard_map/reduce_sum | solution.py:42
  73.8 0.1 reduce_sum.59
  73.9 0.1 reduce_sum.61
  74.0 21.6 %all-reduce = (f32[4,256]{1,0:T(4,128)S(1)}, f32[4,256]{1,0:T(4,128)S(1)}) all-reduce(f32[4,256]{1,0:T(4,128)S(1)} %reduce_sum.61, f32[4,256]{1,0:T(4,128)S(1)} %reduce_sum.59), channel_id=1, replica_groups=mesh['asset'=8,'tm'=4] {'asset'}, use_global_device_ids=true, to_apply=%region_9.10 | all-reduce | flops 2048 | bytes 16384 | tf_op jit(solution)/shard_map/psum | solution.py:47
  95.6 7.9 %fusion.8 = f32[4,256,2048]{2,1,0:T(8,128)} fusion(f32[4,4,64,2048]{3,2,1,0:T(8,128)} %get-tuple-element.18, f32[4,256]{1,0:T(4,128)S(1)} %get-tuple-element.15, f32[4,256]{1,0:T(4,128)S(1)} %get-tuple-element.14, f32[4,256]{1,0:T(4,128)S(1)} %get-tuple-element.17, f32[4,256]{1,0:T(4,128)S(1)} %get-tuple-element.16, f32[256,2048]{1,0:T(8,128)} %maximum_convert_fusion.1, ...), kind=kLoop, calls=%fused_computation.14 | loop fusion | flops 16777216 | bytes 20987904 | tf_op jit(solution)/shard_map/div | solution.py:52
  (13 shorter events, 0.1 us)
Async XLA Ops:
  1.1 5.5 %copy-start.1 = (f32[256,2048]{1,0:T(8,128)}, f32[256,2048]{1,0:T(8,128)S(1)}, u32[]{:S(2)}) copy-start(f32[256,2048]{1,0:T(8,128)S(1)} %and_convert_fusion.1) | copy-start | bytes 6291460
  1.1 7.6 %copy-start.3 = (s32[2048]{0:T(1024)S(1)}, s32[2048]{0:T(1024)}, u32[]{:S(2)}) copy-start(s32[2048]{0:T(1024)} %param.5) | copy-start | bytes 24580
  1.1 7.7 %copy-start.2 = (s32[2048]{0:T(1024)S(1)}, s32[2048]{0:T(1024)}, u32[]{:S(2)}) copy-start(s32[2048]{0:T(1024)} %param.4) | copy-start | bytes 24580
  6.8 27.4 %collective-permute-start = (f32[4,64,2048]{2,1,0:T(8,128)S(1)}, f32[4,64,2048]{2,1,0:T(8,128)S(1)}, u32[]{:S(2)}, u32[]{:S(2)}) collective-permute-start(f32[4,64,2048]{2,1,0:T(8,128)S(1)} %slice.8), channel_id=1, source_target_pairs={{0,1},{1,2},{2,3},{4,5},{5,6},{6,7},{8,9},{9,10},{10,11},{12,13},{... | collective-permute-start | bytes 6291464 | tf_op jit(solution)/shard_map/ppermute | solution.py:12
  12.7 22.8 %copy-start = (f32[4,64,2048]{2,1,0:T(8,128)}, f32[4,64,2048]{2,1,0:T(8,128)S(1)}, u32[]{:S(2)}) copy-start(f32[4,64,2048]{2,1,0:T(8,128)S(1)} %maximum_convert_fusion) | copy-start | bytes 6291460
where the time goes:
time: 104 us
  blocking collectives  40.2 us (39%)
  other arithmetic  24.9 us (24%)
  matrix products  20.4 us (20%)
  waiting for transfers between devices  15.1 us (15%)
  starting transfers between devices  1.92 us (2%)
    psum x1, blocking collectives, standardize(): totals, squares = lax.psum((local_sum, local_sq), 'asset')  21.6 us
    psum x1, blocking collectives, standardize(): lax.psum((count_part, local_sum, local_sq), 'asset')  18.6 us
    ppermute x1, waiting for transfers between devices, passed_along(): return lax.ppermute(block, axis, route)  15.1 us
    dot_general x1, matrix products, window_sums(): within = jnp.einsum('ij,fbja->fbia', lower_band, current, precision=highest)  12.8 us
    div x1, other arithmetic, standardize(): return (deviate / jnp.sqrt(spread + 0.1)[:, :, None], count_total)  7.92 us
    reduce_sum x1, other arithmetic, standardize(): local_sum = jnp.sum(field_values * weight[None], axis=2)  6.55 us
    dot_general x1, matrix products, window_sums(): jnp.einsum('ij,fbja->fbia', upper_band, current[:, :blocks - 1], precisio...  6.31 us
    mul x1, other arithmetic, per_device(): masked = values * weight[None]  5.44 us
  transfers between devices with their start and end apart: 1, of which 1 were waited for; matrix products, arithmetic and copies ran while one was open for 10% of the time, Pallas kernels for 0%

commit v1 on v0

v1 whole, which is shorter than its diff:
```python
import functools

import jax
import jax.numpy as jnp
from jax import lax
from jax.experimental import pallas as pl
from jax.experimental.pallas import tpu as pltpu
from jax.sharding import PartitionSpec as P

WINDOW = 64
LANES = 128
CLIP = 3.0


def kernel(
    n_tm, n_as, values, opened_ref, closed_ref, out,
    x, weight, inverse, part1, part2, total1, total2, got1, got2, tail_part, tail_got,
    load_sem, halo_send, halo_recv, send_sem, recv_sem,
):
    fields, rows, assets = values.shape
    blocks = rows // WINDOW
    chunks = assets // LANES
    items = (blocks - 1) * fields
    tm = lax.axis_index("tm")
    me = lax.axis_index("asset")
    later = lax.rem(tm + 1, n_tm)
    before = lax.rem(tm + n_tm - 1, n_tm)

    loads = [
        pltpu.make_async_copy(values.at[f], x.at[f, pl.ds(WINDOW, rows)], load_sem.at[f])
        for f in range(fields)
    ]
    for copy in loads:
        copy.start()

    barrier = pltpu.get_barrier_semaphore()
    for other in (later, before):
        pl.semaphore_signal(barrier, inc=1, device_id={"tm": other})
    for d in range(1, n_as):
        pl.semaphore_signal(barrier, inc=1, device_id={"asset": lax.rem(me + d, n_as)})
    pl.semaphore_wait(barrier, n_as + 1)

    halos = [
        pltpu.make_async_remote_copy(
            src_ref=values.at[f, pl.ds(rows - WINDOW, WINDOW)],
            dst_ref=x.at[f, pl.ds(0, WINDOW)],
            send_sem=halo_send.at[f],
            recv_sem=halo_recv.at[f],
            device_id={"tm": later},
        )
        for f in range(fields)
    ]
    for copy in halos:
        copy.start()

    def send(part, got, stage):
        for d in range(1, n_as):
            pltpu.make_async_remote_copy(
                src_ref=part,
                dst_ref=got.at[d - 1],
                send_sem=send_sem.at[stage],
                recv_sem=recv_sem.at[stage],
                device_id={"asset": lax.rem(me + d, n_as)},
            ).start()

    def receive(part, got, stage):
        pltpu.make_async_copy(got, got, recv_sem.at[stage]).wait()
        return part[...] + jnp.sum(got[...], axis=0)

    def row_of(first, second):
        return jnp.sum(jnp.concatenate([first, second], axis=0).T, axis=0, keepdims=True)

    def factors(row, count):
        mean = row / jnp.maximum(count, 1.0)
        other = pltpu.roll(mean, WINDOW, 1)
        scale = 1.0 / jnp.sqrt(jnp.maximum(mean - other * other, 0.0) + 0.1)
        lane = lax.broadcasted_iota(jnp.int32, row.shape, 1)
        both = jnp.broadcast_to(jnp.where(lane < WINDOW, mean, scale), (LANES, LANES)).T
        return both[:WINDOW], both[WINDOW:]

    zero = jnp.zeros((WINDOW, LANES), jnp.float32)
    first_stamp = tm * rows - WINDOW

    @pl.loop(0, chunks)
    def listing(c):
        cols = pl.ds(pl.multiple_of(c * LANES, LANES), LANES)
        opened = jnp.maximum(opened_ref[:, cols], 0)
        closed = closed_ref[:, cols]

        @pl.loop(0, blocks + 1)
        def block(b):
            start = pl.multiple_of(b * WINDOW, WINDOW)
            stamps = first_stamp + start + lax.broadcasted_iota(jnp.int32, (WINDOW, LANES), 0)
            listed = (stamps >= opened) & (stamps < closed)
            low = jnp.maximum(stamps - (WINDOW - 1), opened)
            high = jnp.minimum(stamps, closed - 1)
            counted = jnp.maximum(high - low + 1, 1).astype(jnp.float32)
            weight[pl.ds(start, WINDOW), cols] = jnp.where(listed, 1.0, 0.0)
            inverse[pl.ds(start, WINDOW), cols] = jnp.where(listed, 1.0 / counted, 0.0)

    @pl.loop(0, blocks)
    def counting(b):
        def chunk(c, total):
            cols = pl.ds(pl.multiple_of(c * LANES, LANES), LANES)
            return total + weight[pl.ds(pl.multiple_of((b + 1) * WINDOW, WINDOW), WINDOW), cols]

        total = lax.fori_loop(0, chunks, chunk, zero)
        part1[pl.ds(items + b, 1), :] = row_of(total, total)

    def roll_window(f, b):
        top = pl.multiple_of(b * WINDOW, WINDOW)

        def chunk(c, carry):
            cols = pl.ds(pl.multiple_of(c * LANES, LANES), LANES)
            reach = pl.ds(top, 2 * WINDOW)
            sums = x[f, reach, cols] * weight[reach, cols]
            for step in (8, 16, 32):
                sums = sums[step:] + sums[:-step]
            for step in (1, 2, 4):
                sums = sums + pltpu.roll(sums, step, 0)
            rolling = sums[8:] * inverse[pl.ds(top + WINDOW, WINDOW), cols]
            out[f, pl.ds(top, WINDOW), cols] = rolling
            return carry[0] + rolling, carry[1] + rolling * rolling

        return row_of(*lax.fori_loop(0, chunks, chunk, (zero, zero), unroll=2))

    def clip_scores(f, b, center, scale):
        top = pl.multiple_of(b * WINDOW, WINDOW)

        def chunk(c, carry):
            cols = pl.ds(pl.multiple_of(c * LANES, LANES), LANES)
            here = pl.ds(top, WINDOW)
            scored = (out[f, here, cols] - center) * scale
            clipped = jnp.minimum(jnp.maximum(scored, -CLIP), CLIP)
            out[f, here, cols] = clipped
            masked = clipped * weight[pl.ds(top + WINDOW, WINDOW), cols]
            return carry[0] + masked, carry[1] + masked * masked

        return row_of(*lax.fori_loop(0, chunks, chunk, (zero, zero), unroll=2))

    def finish(f, b, center, scale):
        top = pl.multiple_of(b * WINDOW, WINDOW)

        @pl.loop(0, chunks, unroll=2)
        def chunk(c):
            cols = pl.ds(pl.multiple_of(c * LANES, LANES), LANES)
            here = pl.ds(top, WINDOW)
            deviate = (out[f, here, cols] - center) * weight[pl.ds(top + WINDOW, WINDOW), cols]
            out[f, here, cols] = deviate * scale

    for f in range(fields):
        loads[f].wait()

        @pl.loop(1, blocks)
        def windows(b):
            part1[pl.ds((b - 1) * fields + f, 1), :] = roll_window(f, b)

    send(part1, got1, 0)

    def main_second():
        total1[...] = receive(part1, got1, 0)

        @pl.loop(0, items)
        def item(i):
            b = lax.div(i, fields) + 1
            f = lax.rem(i, fields)
            count = total1[pl.ds(items + b, 1), :]
            center, scale = factors(total1[pl.ds(i, 1), :], count)
            part2[pl.ds(i, 1), :] = clip_scores(f, b, center, scale)

        send(part2, got2, 1)

    def main_third():
        total2[...] = receive(part2, got2, 1)

        @pl.loop(0, items)
        def item(i):
            b = lax.div(i, fields) + 1
            f = lax.rem(i, fields)
            count = total1[pl.ds(items + b, 1), :]
            center, scale = factors(total2[pl.ds(i, 1), :], count)
            finish(f, b, center, scale)

    def tail_first(f):
        halos[f].wait_recv()
        tail_part[2 * f] = jnp.broadcast_to(roll_window(f, 0), (8, LANES))
        send(tail_part.at[2 * f], tail_got.at[2 * f], 2 + 2 * f)

    def tail_factors(f, part):
        slot = 2 * f + part
        row = receive(tail_part.at[slot], tail_got.at[slot], 2 + slot)[:1]
        return factors(row, total1[pl.ds(items, 1), :])

    def tail_second(f):
        row = clip_scores(f, 0, *tail_factors(f, 0))
        tail_part[2 * f + 1] = jnp.broadcast_to(row, (8, LANES))
        send(tail_part.at[2 * f + 1], tail_got.at[2 * f + 1], 3 + 2 * f)

    def tail_third(f):
        finish(f, 0, *tail_factors(f, 1))

    tail_first(0)
    main_second()
    if fields > 1:
        tail_first(1)
    tail_second(0)
    main_third()
    for f in range(2, fields):
        tail_first(f)
        tail_second(f - 1)
        tail_third(f - 2)
    if fields > 1:
        tail_second(fields - 1)
        tail_third(fields - 2)
    tail_third(fields - 1)

    for copy in halos:
        copy.wait_send()
    pltpu.make_async_copy(got1, got1, send_sem.at[0]).wait()
    pltpu.make_async_copy(got2, got2, send_sem.at[1]).wait()
    for slot in range(2 * fields):
        got = tail_got.at[slot]
        pltpu.make_async_copy(got, got, send_sem.at[2 + slot]).wait()


def per_device(n_tm, n_as, values, listed_from, listed_until):
    fields, rows, assets = values.shape
    blocks = rows // WINDOW
    stats = -(-((blocks - 1) * fields + blocks) // 8) * 8
    f32 = jnp.float32
    vmem = pltpu.VMEM
    dma = pltpu.SemaphoreType.DMA
    return pl.pallas_call(
        functools.partial(kernel, n_tm, n_as),
        out_shape=vmem((fields, rows, assets), f32),
        in_specs=[
            pl.BlockSpec(memory_space=pl.ANY),
            pl.BlockSpec(memory_space=vmem),
            pl.BlockSpec(memory_space=vmem),
        ],
        out_specs=pl.BlockSpec(memory_space=vmem),
        scratch_shapes=[
            vmem((fields, WINDOW + rows, assets), f32),
            vmem((WINDOW + rows, assets), f32),
            vmem((WINDOW + rows, assets), f32),
            vmem((stats, LANES), f32),
            vmem((stats, LANES), f32),
            vmem((stats, LANES), f32),
            vmem((stats, LANES), f32),
            vmem((n_as - 1, stats, LANES), f32),
            vmem((n_as - 1, stats, LANES), f32),
            vmem((2 * fields, 8, LANES), f32),
            vmem((2 * fields, n_as - 1, 8, LANES), f32),
            dma((fields,)),
            dma((fields,)),
            dma((fields,)),
            dma((2 + 2 * fields,)),
            dma((2 + 2 * fields,)),
        ],
        compiler_params=pltpu.CompilerParams(
            collective_id=0, has_side_effects=True, vmem_limit_bytes=40 * 2**20
        ),
    )(values, listed_from[None], listed_until[None])


def solution(mesh):
    in_specs = (P(None, "tm", "asset"), P("asset"), P("asset"))
    out_specs = P(None, "tm", "asset")
    body = functools.partial(per_device, mesh.shape["tm"], mesh.shape["asset"])
    return jax.shard_map(
        body, mesh=mesh, in_specs=in_specs, out_specs=out_specs, check_vma=False
    )
```

time: 104 us -> 53.4 us (0.51)
  the two profiles are of different devices: /device:TPU:6 before, /device:TPU:0 now
where the time goes in v1:
time: 53.4 us; the launch traced here: 53.1 us
  Pallas kernels  48.3 us (90%)
  local copies, waits for them, and re-layouts  4.79 us (9%)
    pallas_call x1, Pallas kernels, per_device(): pl.pallas_call(functools.partial(kernel, n_tm, n_as), out_shape=vmem((fie...  48.3 us
    unnamed x5, local copies, waits for them, and re-layouts  4.79 us

profile of v1, /device:TPU:0, one launch (start us, length us, event | category | flops | bytes accessed | tf_op | source)
XLA Modules:
  0.0 53.1 jit_solution(5567783908357812001)
XLA Ops:
  0.0 0.0 copy-start
  0.0 0.7 %copy-done = s32[2048]{0:T(1024)S(1)} copy-done((s32[2048]{0:T(1024)S(1)}, s32[2048]{0:T(1024)}, u32[]{:S(2)}) %copy-start) | copy-done | bytes 8216
  0.7 0.0 copy-start.1
  0.7 0.7 %copy-done.1 = s32[2048]{0:T(1024)S(1)} copy-done((s32[2048]{0:T(1024)S(1)}, s32[2048]{0:T(1024)}, u32[]{:S(2)}) %copy-start.1) | copy-done | bytes 8216
  1.4 48.3 %shard_map.37 = f32[4,256,2048]{2,1,0:T(8,128)S(1)} custom-call(f32[4,256,2048]{2,1,0:T(8,128)} %values.1, s32[1,2048]{1,0:T(1,128)S(1)} %bitcast.2, s32[1,2048]{1,0:T(1,128)S(1)} %bitcast.3), custom_call_target="tpu_custom_call" | custom-call | tf_op jit(solution)/shard_map/pallas_call | solution.py:233
  49.7 3.4 %copy.5 = f32[4,256,2048]{2,1,0:T(8,128)} copy(f32[4,256,2048]{2,1,0:T(8,128)S(1)} %shard_map.37) | data formatting | bytes 16777216
Async XLA Ops:
  0.0 0.7 %copy-start = (s32[2048]{0:T(1024)S(1)}, s32[2048]{0:T(1024)}, u32[]{:S(2)}) copy-start(s32[2048]{0:T(1024)} %param.4) | copy-start | bytes 24580
  0.7 0.7 %copy-start.1 = (s32[2048]{0:T(1024)S(1)}, s32[2048]{0:T(1024)}, u32[]{:S(2)}) copy-start(s32[2048]{0:T(1024)} %param.5) | copy-start | bytes 24580

commit v2 on v1

v2 whole, which is shorter than its diff:
```python
import functools

import jax
import jax.numpy as jnp
from jax import lax
from jax.experimental import pallas as pl
from jax.experimental.pallas import tpu as pltpu
from jax.sharding import PartitionSpec as P

WINDOW = 64
LANES = 128
CLIP = 3.0
UNROLL = 4


def field_groups(fields):
    half = (fields + 1) // 2
    return [(start, min(half, fields - start)) for start in range(0, fields, half)]


def kernel(
    n_tm, n_as, values, opened_hbm, closed_hbm, out,
    x, rolling, weight, inverse, opened_ref, closed_ref, part, got, totals,
    load_sem, halo_send, halo_recv, send_sem, recv_sem,
):
    fields, rows, assets = values.shape
    blocks = rows // WINDOW
    chunks = assets // LANES
    groups = field_groups(fields)
    tm = lax.axis_index("tm")
    me = lax.axis_index("asset")
    later = lax.rem(tm + 1, n_tm)
    before = lax.rem(tm + n_tm - 1, n_tm)

    dates = [
        pltpu.make_async_copy(opened_hbm, opened_ref, load_sem.at[fields]),
        pltpu.make_async_copy(closed_hbm, closed_ref, load_sem.at[fields + 1]),
    ]
    loads = [
        pltpu.make_async_copy(values.at[f], x.at[f, pl.ds(WINDOW, rows)], load_sem.at[f])
        for f in range(fields)
    ]

    barrier = pltpu.get_barrier_semaphore()
    for other in (later, before):
        pl.semaphore_signal(barrier, inc=1, device_id={"tm": other})
    for d in range(1, n_as):
        pl.semaphore_signal(barrier, inc=1, device_id={"asset": lax.rem(me + d, n_as)})
    for copy in dates + loads:
        copy.start()
    pl.semaphore_wait(barrier, n_as + 1)

    halos = [
        pltpu.make_async_remote_copy(
            src_ref=values.at[f, pl.ds(rows - WINDOW, WINDOW)],
            dst_ref=x.at[f, pl.ds(0, WINDOW)],
            send_sem=halo_send.at[f],
            recv_sem=halo_recv.at[f],
            device_id={"tm": later},
        )
        for f in range(fields)
    ]
    for copy in halos:
        copy.start()

    def send(slot):
        for d in range(1, n_as):
            pltpu.make_async_remote_copy(
                src_ref=part.at[slot],
                dst_ref=got.at[slot, d - 1],
                send_sem=send_sem.at[slot],
                recv_sem=recv_sem.at[slot],
                device_id={"asset": lax.rem(me + d, n_as)},
            ).start()

    def receive(slot):
        arrived = got.at[slot]
        pltpu.make_async_copy(arrived, arrived, recv_sem.at[slot]).wait()
        return part[slot] + jnp.sum(got[slot], axis=0)

    def row_of(first, second):
        return jnp.sum(jnp.concatenate([first, second], axis=0).T, axis=0, keepdims=True)

    def factors(row, count):
        mean = row / jnp.maximum(count, 1.0)
        other = pltpu.roll(mean, WINDOW, 1)
        scale = 1.0 / jnp.sqrt(jnp.maximum(mean - other * other, 0.0) + 0.1)
        lane = lax.broadcasted_iota(jnp.int32, row.shape, 1)
        both = jnp.broadcast_to(jnp.where(lane < WINDOW, mean, scale), (LANES, LANES)).T
        return both[:WINDOW], both[WINDOW:]

    def columns(c):
        return pl.ds(pl.multiple_of(c * LANES, LANES), LANES)

    zero = jnp.zeros((WINDOW, LANES), jnp.float32)
    part[...] = jnp.zeros(part.shape, part.dtype)
    first_stamp = tm * rows - WINDOW
    for copy in dates:
        copy.wait()

    @pl.loop(0, blocks + 1)
    def listing(b):
        start = pl.multiple_of(b * WINDOW, WINDOW)
        stamps = first_stamp + start + lax.broadcasted_iota(jnp.int32, (WINDOW, LANES), 0)

        def chunk(c, total):
            cols = columns(c)
            opened = jnp.maximum(opened_ref[:, cols], 0)
            closed = closed_ref[:, cols]
            listed = (stamps >= opened) & (stamps < closed)
            low = jnp.maximum(stamps - (WINDOW - 1), opened)
            counted = jnp.maximum(jnp.minimum(stamps + 1, closed) - low, 1).astype(jnp.float32)
            ones = jnp.where(listed, 1.0, 0.0)
            weight[pl.ds(start, WINDOW), cols] = ones
            inverse[pl.ds(start, WINDOW), cols] = ones / counted
            return total + ones

        total = lax.fori_loop(0, chunks, chunk, zero, unroll=2)
        part[0, pl.ds(lax.rem(b + blocks, blocks + 1), 1), :] = row_of(total, total)

    send(0)

    def roll_window(f, b):
        top = pl.multiple_of(b * WINDOW, WINDOW)

        def chunk(c, carry):
            cols = columns(c)
            reach = pl.ds(top, 2 * WINDOW)
            sums = x[f, reach, cols] * weight[reach, cols]
            for step in (8, 16, 32):
                sums = sums[step:] + sums[:-step]
            for step in (1, 2, 4):
                sums = sums + pltpu.roll(sums, step, 0)
            means = sums[8:] * inverse[pl.ds(top + WINDOW, WINDOW), cols]
            rolling[f, pl.ds(top, WINDOW), cols] = means
            return carry[0] + means, carry[1] + means * means

        return row_of(*lax.fori_loop(0, chunks, chunk, (zero, zero), unroll=UNROLL))

    def clip_scores(f, b, center, scale):
        top = pl.multiple_of(b * WINDOW, WINDOW)

        def chunk(c, carry):
            cols = columns(c)
            scored = (rolling[f, pl.ds(top, WINDOW), cols] - center) * scale
            clipped = jnp.minimum(jnp.maximum(scored, -CLIP), CLIP)
            masked = clipped * weight[pl.ds(top + WINDOW, WINDOW), cols]
            return carry[0] + masked, carry[1] + masked * clipped

        return row_of(*lax.fori_loop(0, chunks, chunk, (zero, zero), unroll=UNROLL))

    def finish(f, b, first, second):
        top = pl.multiple_of(b * WINDOW, WINDOW)
        center, scale = first
        middle, factor = second

        @pl.loop(0, chunks, unroll=UNROLL)
        def chunk(c):
            cols = columns(c)
            here = pl.ds(top, WINDOW)
            scored = (rolling[f, here, cols] - center) * scale
            clipped = jnp.minimum(jnp.maximum(scored, -CLIP), CLIP)
            deviate = (clipped - middle) * weight[pl.ds(top + WINDOW, WINDOW), cols]
            out[f, here, cols] = deviate * factor

    def count_row(b):
        return totals[0, pl.ds(b, 1), :]

    def total_row(slot, i):
        return totals[slot, pl.ds(i, 1), :]

    def main_first(g):
        start, size = groups[g]
        for f in range(start, start + size):
            loads[f].wait()

        @pl.loop(0, size * (blocks - 1))
        def item(i):
            f, b = start + lax.rem(i, size), 1 + lax.div(i, size)
            part[1 + 2 * g, pl.ds(i, 1), :] = roll_window(f, b)

        send(1 + 2 * g)

    def main_second(g):
        start, size = groups[g]
        slot = 1 + 2 * g
        totals[slot] = receive(slot)

        @pl.loop(0, size * (blocks - 1))
        def item(i):
            f, b = start + lax.rem(i, size), 1 + lax.div(i, size)
            center, scale = factors(total_row(slot, i), count_row(b))
            part[slot + 1, pl.ds(i, 1), :] = clip_scores(f, b, center, scale)

        send(slot + 1)

    def main_third(g):
        start, size = groups[g]
        slot = 1 + 2 * g
        totals[slot + 1] = receive(slot + 1)

        @pl.loop(0, size * (blocks - 1))
        def item(i):
            f, b = start + lax.rem(i, size), 1 + lax.div(i, size)
            count = count_row(b)
            first = factors(total_row(slot, i), count)
            finish(f, b, first, factors(total_row(slot + 1, i), count))

    tail_slot = 1 + 2 * len(groups)

    def tail_first(f):
        slot = tail_slot + 2 * f
        halos[f].wait_recv()
        part[slot, :1, :] = roll_window(f, 0)
        send(slot)

    def tail_second(f):
        slot = tail_slot + 2 * f
        totals[slot] = receive(slot)
        center, scale = factors(total_row(slot, 0), count_row(0))
        part[slot + 1, :1, :] = clip_scores(f, 0, center, scale)
        send(slot + 1)

    def tail_third(f):
        slot = tail_slot + 2 * f
        totals[slot + 1] = receive(slot + 1)
        first = factors(total_row(slot, 0), count_row(0))
        finish(f, 0, first, factors(total_row(slot + 1, 0), count_row(0)))

    early = min(2, fields)
    for g in range(len(groups)):
        main_first(g)
    totals[0] = receive(0)
    for step in range(max(early, len(groups))):
        if step < early:
            tail_first(step)
        if step < len(groups):
            main_second(step)
    for step in range(max(early, len(groups))):
        if step < early:
            tail_second(step)
        if step < len(groups):
            main_third(step)
    for f in range(early, fields):
        tail_first(f)
        if f > early:
            tail_second(f - 1)
        tail_third(f - early)
    if fields > early:
        tail_second(fields - 1)
    for f in range(fields - early, fields):
        tail_third(f)

    for copy in halos:
        copy.wait_send()
    for slot in range(part.shape[0]):
        sent = got.at[slot]
        pltpu.make_async_copy(sent, sent, send_sem.at[slot]).wait()


def per_device(n_tm, n_as, values, listed_from, listed_until):
    fields, rows, assets = values.shape
    blocks = rows // WINDOW
    groups = field_groups(fields)
    stats = -(-max(groups[0][1] * (blocks - 1), blocks + 1) // 8) * 8
    slots = 1 + 2 * len(groups) + 2 * fields
    f32 = jnp.float32
    vmem = pltpu.VMEM
    dma = pltpu.SemaphoreType.DMA
    return pl.pallas_call(
        functools.partial(kernel, n_tm, n_as),
        out_shape=vmem((fields, rows, assets), f32),
        in_specs=[pl.BlockSpec(memory_space=pltpu.HBM)] * 3,
        out_specs=pl.BlockSpec(memory_space=vmem),
        scratch_shapes=[
            vmem((fields, WINDOW + rows, assets), f32),
            vmem((fields, rows, assets), f32),
            vmem((WINDOW + rows, assets), f32),
            vmem((WINDOW + rows, assets), f32),
            vmem((1, assets), jnp.int32),
            vmem((1, assets), jnp.int32),
            vmem((slots, stats, LANES), f32),
            vmem((slots, n_as - 1, stats, LANES), f32),
            vmem((slots, stats, LANES), f32),
            dma((fields + 2,)),
            dma((fields,)),
            dma((fields,)),
            dma((slots,)),
            dma((slots,)),
        ],
        compiler_params=pltpu.CompilerParams(
            collective_id=0, has_side_effects=True, vmem_limit_bytes=48 * 2**20
        ),
    )(values, listed_from[None], listed_until[None])


def solution(mesh):
    in_specs = (P(None, "tm", "asset"), P("asset"), P("asset"))
    out_specs = P(None, "tm", "asset")
    body = functools.partial(per_device, mesh.shape["tm"], mesh.shape["asset"])
    return jax.shard_map(
        body, mesh=mesh, in_specs=in_specs, out_specs=out_specs, check_vma=False
    )
```

time: 53.4 us -> 44.1 us (0.83)
  Pallas kernels: 48.3 us -> 40.6 us
  local copies, waits for them, and re-layouts: 4.79 us -> 3.4 us
    pallas_call x1, Pallas kernels: 48.3 us -> 40.6 us  [per_device(): pl.pallas_call(functools.partial(kernel, n_tm, n_as), out_shape=vmem((fie...]
    unnamed x5 -> x1, local copies, waits for them, and re-layouts: 4.79 us -> 3.4 us
where the time goes in v2:
time: 44.1 us; the launch traced here: 44 us
  Pallas kernels  40.6 us (92%)
  local copies, waits for them, and re-layouts  3.4 us (8%)
    pallas_call x1, Pallas kernels, per_device(): pl.pallas_call(functools.partial(kernel, n_tm, n_as), out_shape=vmem((fie...  40.6 us
    unnamed x1, local copies, waits for them, and re-layouts  3.4 us

profile of v2, /device:TPU:0, one launch (start us, length us, event | category | flops | bytes accessed | tf_op | source)
XLA Modules:
  0.0 44.0 jit_solution(13742465517196990218)
XLA Ops:
  0.0 40.6 %shard_map.37 = f32[4,256,2048]{2,1,0:T(8,128)S(1)} custom-call(f32[4,256,2048]{2,1,0:T(8,128)} %values.1, s32[1,2048]{1,0:T(1,128)} %bitcast.2, s32[1,2048]{1,0:T(1,128)} %bitcast.3), custom_call_target="tpu_custom_call" | custom-call | tf_op jit(solution)/shard_map/pallas_call | solution.py:270
  40.6 3.4 %copy.5 = f32[4,256,2048]{2,1,0:T(8,128)} copy(f32[4,256,2048]{2,1,0:T(8,128)S(1)} %shard_map.37) | data formatting | bytes 16777216
